TPU v7x, 128 devices: a whole 4x4x4 slice. The times are simulated.
128 devices in a mesh: block: 2 (over z_lo), span: 8 (over y, x_lo), group: 8 (over z_hi, x_hi, core).
Axes of the slice: x: 4 (x_hi: 2, x_lo: 2; x = x_hi * 2 + x_lo), y: 4, z: 4 (z_hi: 2, z_lo: 2; z = z_hi * 2 + z_lo), core: 2. Of those that a mesh axis runs over, the one named last changes fastest.
Arguments:
- key_rows: bfloat16 [16, 24576, 8, 128], P(None, ('block', 'span'), 'group'), may hold values from -6 to 6
- value_rows: bfloat16 [16, 24576, 8, 128], P(None, ('block', 'span'), 'group'), may hold values from -6 to 6
- turn_angle: float32 [24576, 64], replicated, may hold values from -3.140625 to 3.140625
- key_gain: float32 [128], replicated, may hold values from 0.25 to 1.75
Outputs:
- stored_keys: bfloat16 [16, 8, 128, 24576], P(('block', 'span'), 'group')
- stored_values: bfloat16 [16, 24576, 8, 128], P(('block', 'span'), None, 'group')
- key_scale: float32 [16, 8, 128], P(('block', 'span'), 'group')
All inputs are finite; a program needn't handle non-finite values. Where the computation divides by a largest or mean magnitude, that divisor is 1e-20 or more.
Results may differ from a plain program's by a relative error of at most 0.001.
Values may be sent and summed in bfloat16 or wider, within the bound.
A program may use at most 128 MiB of HBM per device.

v0:
```python
import jax
import jax.numpy as jnp
from jax import lax
from jax.sharding import PartitionSpec as P


def apply_rotary(vectors, angle):
    half = vectors.shape[-1] // 2
    cosine, sine = (jnp.cos(angle)[None, :, None, :], jnp.sin(angle)[None, :, None, :])
    first, second = (vectors[..., :half], vectors[..., half:])
    return jnp.concatenate(
        [first * cosine - second * sine, second * cosine + first * sine], axis=-1
    )


def unit_rows(vectors, row_gain):
    return (
        vectors * lax.rsqrt(jnp.mean(vectors * vectors, axis=-1, keepdims=True) + 1e-06) * row_gain
    )


def ready_to_store(plain_keys, angle, key_gain):
    wide_keys = plain_keys.astype(jnp.float32)
    wide_keys = unit_rows(wide_keys, key_gain)
    return apply_rotary(wide_keys, angle)


def body(key_rows, value_rows, turn_angle, key_gain):
    moved_keys, stored_values = (
        lax.all_to_all(key_rows, ("block", "span"), split_axis=0, concat_axis=1, tiled=True),
        lax.all_to_all(value_rows, ("block", "span"), split_axis=0, concat_axis=1, tiled=True),
    )
    turned_keys = ready_to_store(moved_keys, turn_angle, key_gain)
    key_scale = jnp.max(jnp.abs(turned_keys), axis=1)
    narrow_keys = (turned_keys / key_scale[:, None]).astype(jnp.bfloat16)
    stored_keys = jnp.transpose(narrow_keys, (0, 2, 3, 1))
    return (stored_keys, stored_values, key_scale)


def solution(mesh):
    return jax.shard_map(
        body,
        mesh=mesh,
        in_specs=(
            P(None, ("block", "span"), "group", None),
            P(None, ("block", "span"), "group", None),
            P(),
            P(),
        ),
        out_specs=(
            P(("block", "span"), "group", None, None),
            P(("block", "span"), None, "group", None),
            P(("block", "span"), "group", None),
        ),
        check_vma=False,
    )
```

profile of v0, /device:TPU:1, one launch (start us, length us, event | category | flops | bytes accessed | tf_op | source)
XLA Modules:
  0.0 210.6 jit_solution(14011961175013457395)
XLA Ops:
  0.6 7.5 %all-to-all-start = ((bf16[16,1536,1,128]{3,1,2,0:T(8,128)(2,1)}), bf16[16,1536,1,128]{3,1,2,0:T(8,128)(2,1)}, u32[]{:S(2)}, u32[]{:S(2)}) async-start(bf16[16,1536,1,128]{3,1,2,0:T(8,128)(2,1)} %param.4), calls=%async_computation | async-start | bytes 12582912 | tf_op jit(solution)/shard_map/all_to_all | solution.py:30
  8.1 24.1 %fusion.3 = (f32[24576,64]{0,1:T(8,128)}, f32[24576,64]{0,1:T(8,128)}) fusion(f32[24576,64]{0,1:T(8,128)} %param.6), kind=kLoop, calls=%fused_computation.13 | loop fusion | bytes 18874368 | tf_op jit(solution)/shard_map/cos | solution.py:9
  32.2 72.5 %all-to-all-done = bf16[16,1536,1,128]{3,1,2,0:T(8,128)(2,1)} async-done(((bf16[16,1536,1,128]{3,1,2,0:T(8,128)(2,1)}), bf16[16,1536,1,128]{3,1,2,0:T(8,128)(2,1)}, u32[]{:S(2)}, u32[]{:S(2)}) %all-to-all-start) | async-done | bytes 6291488 | tf_op jit(solution)/shard_map/all_to_all | solution.py:30
  104.8 4.6 %all-to-all-start.1 = ((bf16[16,1536,1,128]{3,1,2,0:T(8,128)(2,1)}), bf16[16,1536,1,128]{3,1,2,0:T(8,128)(2,1)}, u32[]{:S(2)}, u32[]{:S(2)}) async-start(bf16[16,1536,1,128]{3,1,2,0:T(8,128)(2,1)} %param.5), calls=%async_computation.1 | async-start | bytes 12582912 | tf_op jit(solution)/shard_map/all_to_all | solution.py:31
  109.4 9.5 %copy.8 = f32[1,24576,1,128]{1,3,2,0:T(8,128)} copy(bf16[1,24576,1,128]{3,1,2,0:T(8,128)(2,1)} %bitcast.19) | data formatting | bytes 18874368 | tf_op jit(solution)/shard_map/convert_element_type | solution.py:23
  118.9 0.0 copy-start.1
  118.9 6.1 %multiply_reduce_fusion = f32[16,1536]{1,0:T(8,128)S(1)} fusion(bf16[16,1536,1,128]{3,1,2,0:T(8,128)(2,1)} %all-to-all-done), kind=kLoop, calls=%fused_computation.4 | loop fusion | flops 9412608 | bytes 6389760 | tf_op jit(solution)/shard_map/reduce_sum | solution.py:18
  125.1 0.0 copy-done.1
  125.1 10.5 %multiply_multiply_fusion = f32[1,24576,1,128]{1,3,2,0:T(8,128)} fusion(f32[1,24576,1,128]{1,3,2,0:T(8,128)} %copy.8, f32[128]{0:T(128)S(1)} %copy-done.1, f32[24576]{0:T(1024)S(1)} %rsqrt.12), kind=kLoop, calls=%fused_computation.3 | loop fusion | flops 6291456 | bytes 25264640 | tf_op jit(solution)/shard_map/mul | solution.py:18
  135.6 11.7 %fusion = (f32[1,24576,1,64]{1,3,2,0:T(8,128)S(1)}, f32[1,24576,1,64]{1,3,2,0:T(8,128)}) fusion(f32[24576,64]{0,1:T(8,128)} %get-tuple-element.6, f32[24576,64]{0,1:T(8,128)} %get-tuple-element.5, f32[1,24576,1,128]{1,3,2,0:T(8,128)} %multiply_multiply_fusion), kind=kLoop, calls=%fused_computation.7 | loop fusion | flops 9437184 | bytes 37748736 | tf_op jit(solution)/shard_map/sub | solution.py:12
  147.3 4.0 %abs_reduce_fusion = f32[128]{0:T(128)S(1)} fusion(f32[1,24576,1,64]{1,3,2,0:T(8,128)} %get-tuple-element.4, f32[1,24576,1,64]{1,3,2,0:T(8,128)S(1)} %get-tuple-element.3), kind=kLoop, calls=%fused_computation.2 | loop fusion | flops 9437056 | bytes 12583424 | tf_op jit(solution)/shard_map/reduce_max | solution.py:34
  151.3 0.0 copy-start
  151.3 6.9 %fusion.2 = bf16[1,1,128,24576]{3,2,1,0:T(8,128)(2,1)} fusion(f32[128]{0:T(128)S(1)} %abs_reduce_fusion, f32[1,24576,1,64]{1,3,2,0:T(8,128)} %get-tuple-element.4, f32[1,24576,1,64]{1,3,2,0:T(8,128)S(1)} %get-tuple-element.3), kind=kLoop, calls=%fused_computation.11 | loop fusion | flops 9437184 | bytes 18874880 | tf_op jit(solution)/shard_map/transpose | solution.py:36
  158.3 0.0 copy-done
  158.3 45.9 %all-to-all-done.1 = bf16[16,1536,1,128]{3,1,2,0:T(8,128)(2,1)} async-done(((bf16[16,1536,1,128]{3,1,2,0:T(8,128)(2,1)}), bf16[16,1536,1,128]{3,1,2,0:T(8,128)(2,1)}, u32[]{:S(2)}, u32[]{:S(2)}) %all-to-all-start.1) | async-done | bytes 6291488 | tf_op jit(solution)/shard_map/all_to_all | solution.py:31
  204.2 6.4 %copy.10 = bf16[1,24576,1,128]{3,1,2,0:T(8,128)(2,1)} copy(bf16[1,24576,1,128]{3,1,2,0:T(8,128)(2,1)} %bitcast.4) | data formatting | bytes 12582912
  (2 shorter events, 0.0 us)
Async XLA Ops:
  0.6 104.1 %all-to-all-start = ((bf16[16,1536,1,128]{3,1,2,0:T(8,128)(2,1)}), bf16[16,1536,1,128]{3,1,2,0:T(8,128)(2,1)}, u32[]{:S(2)}, u32[]{:S(2)}) async-start(bf16[16,1536,1,128]{3,1,2,0:T(8,128)(2,1)} %param.4), calls=%async_computation | async-start | bytes 12582912 | tf_op jit(solution)/shard_map/all_to_all | solution.py:30
  104.8 99.4 %all-to-all-start.1 = ((bf16[16,1536,1,128]{3,1,2,0:T(8,128)(2,1)}), bf16[16,1536,1,128]{3,1,2,0:T(8,128)(2,1)}, u32[]{:S(2)}, u32[]{:S(2)}) async-start(bf16[16,1536,1,128]{3,1,2,0:T(8,128)(2,1)} %param.5), calls=%async_computation.1 | async-start | bytes 12582912 | tf_op jit(solution)/shard_map/all_to_all | solution.py:31
  118.9 6.2 %copy-start.1 = (f32[128]{0:T(128)S(1)}, f32[128]{0:T(128)}, u32[]{:S(2)}) copy-start(f32[128]{0:T(128)} %param.7) | copy-start | bytes 1540
  151.3 6.9 %copy-start = (f32[128]{0:T(128)}, f32[128]{0:T(128)S(1)}, u32[]{:S(2)}) copy-start(f32[128]{0:T(128)S(1)} %abs_reduce_fusion) | copy-start | bytes 1540
where the time goes:
time: 212 us; the launch traced here: 211 us
  waiting for transfers between devices  118 us (56%)
  local copies, waits for them, and re-layouts  40 us (19%)
  other arithmetic  39.3 us (19%)
  starting transfers between devices  12.1 us (6%)
    all_to_all x1, waiting for transfers between devices, body(): lax.all_to_all(key_rows, ('block', 'span'), split_axis=0, concat_axis=1,...  72.5 us
    all_to_all x1, waiting for transfers between devices, body(): lax.all_to_all(value_rows, ('block', 'span'), split_axis=0, concat_axis=1...  45.9 us
    cos x1, local copies, waits for them, and re-layouts, apply_rotary(): jnp.cos(angle)[None, :, None, :]  24.1 us
    sub x1, other arithmetic, apply_rotary(): first * cosine - second * sine  11.7 us
    mul x1, other arithmetic, unit_rows(): vectors * lax.rsqrt(jnp.mean(vectors * vectors, axis=-1, keepdims=True) +...  10.5 us
    convert_element_type x1, local copies, waits for them, and re-layouts, ready_to_store(): wide_keys = plain_keys.astype(jnp.float32)  9.46 us
    all_to_all x1, starting transfers between devices, body(): lax.all_to_all(key_rows, ('block', 'span'), split_axis=0, concat_axis=1,...  7.45 us
    transpose x1, other arithmetic, body(): stored_keys = jnp.transpose(narrow_keys, (0, 2, 3, 1))  6.93 us
  transfers between devices with their start and end apart: 2, of which 2 were waited for; matrix products, arithmetic and copies ran while one was open for 35% of the time, Pallas kernels for 0%

commit v1 on v0

v1 whole, which is shorter than its diff:
```python
import functools

import jax
import jax.numpy as jnp
from jax import lax
from jax.experimental import pallas as pl
from jax.experimental.pallas import tpu as pltpu
from jax.sharding import PartitionSpec as P

MESH = pl.DeviceIdType.MESH
ORDER = ("xzy", "zyx", "yxz")
STEP = {"x": (1, 0, 0), "z": (0, 0, 1), "p": (0, 1, 0), "m": (0, 3, 0)}
OFFSETS = [(x, y, z) for x in range(2) for y in range(4) for z in range(2) if x or y or z]
TILE = 128


def path(offset, order):
    dx, dy, dz = offset
    links = {
        "x": ["x"] * dx,
        "z": ["z"] * dz,
        "y": [[], ["p"], ["p", "p"] if (dx + dz) % 2 == 0 else ["m", "m"], ["m"]][dy],
    }
    return [link for axis in order for link in links[axis]]


def plan():
    hops = []
    for array in range(2):
        for strip, order in enumerate(ORDER):
            for phase, axis in enumerate(order):
                for link in "pm" if axis == "y" else axis:
                    items = []
                    for offset in OFFSETS:
                        links = path(offset, order)
                        for at, name in enumerate(links):
                            if name == link:
                                again = at > 0 and links[at - 1] == link
                                first = link in "pm" and offset[1] == 2 and not again
                                left = len(links) - at - 1
                                key = (4 * again - first, at > again, -left)
                                items.append((key, offset, at, left == 0))
                    for i, (_, offset, at, last) in enumerate(sorted(items)):
                        hops.append(
                            dict(
                                array=array,
                                strip=strip,
                                offset=offset,
                                at=at,
                                link=link,
                                last=last,
                                time=(array * 3 + phase) * 8 + i,
                                done=path(offset, order)[:at],
                            )
                        )
    hops.sort(key=lambda h: (h["time"], "xzpm".index(h["link"])))
    where = {(h["array"], h["strip"], h["offset"], h["at"]): i for i, h in enumerate(hops)}
    slots = 0
    for h in hops:
        h["after"] = where[h["array"], h["strip"], h["offset"], h["at"] - 1] if h["at"] else None
        h["slot"] = None
        if not h["last"]:
            h["slot"], slots = slots, slots + 1
    return hops, slots


def kernel(
    hops, angle, gain, keys, values, out_keys, out_values, out_scale,
    raw, table, transit, gains, top, send, recv, local,
):
    blocks, rows, size = raw.shape
    half = size // 2
    length = blocks * rows
    strip_rows = rows // len(ORDER)
    z = lax.axis_index("block")
    y = lax.axis_index("span") // 2
    x = lax.axis_index("span") % 2

    def device(step):
        return {"block": (z + step[2]) % 2, "span": ((y + step[1]) % 4) * 2 + (x + step[0]) % 2}

    def block_at(dx, dy, dz):
        return ((z + dz) % 2) * 8 + ((y + dy) % 4) * 2 + (x + dx) % 2

    barrier = pltpu.get_barrier_semaphore()
    for step in STEP.values():
        pl.semaphore_signal(barrier, inc=1, device_id=device(step), device_id_type=MESH)
    pl.semaphore_wait(barrier, len(STEP))

    copies = [None] * len(hops)
    received = set()

    def arrived(i):
        if i not in received:
            copies[i].wait_recv()
            received.add(i)

    def start(i):
        hop = hops[i]
        span = pl.ds(hop["strip"] * strip_rows, strip_rows)
        if hop["after"] is None:
            source = (keys, values)[hop["array"]].at[block_at(*hop["offset"]), span]
        else:
            arrived(hop["after"])
            source = transit.at[hops[hop["after"]]["slot"]]
        if hop["last"]:
            gone = [sum(STEP[link][axis] for link in hop["done"]) for axis in range(3)]
            target = (raw, out_values)[hop["array"]].at[
                block_at(gone[0], 8 - gone[1], gone[2]), span
            ]
        else:
            target = transit.at[hop["slot"]]
        copies[i] = pltpu.make_async_remote_copy(
            src_ref=source,
            dst_ref=target,
            send_sem=send.at[i],
            recv_sem=recv.at[i],
            device_id=device(STEP[hop["link"]]),
            device_id_type=MESH,
        )
        copies[i].start()

    me = block_at(0, 0, 0)
    angles_in = pltpu.make_async_copy(angle, table.at[pl.ds(0, half)], local.at[0])
    keys_in = pltpu.make_async_copy(keys.at[me], raw.at[me], local.at[1])
    values_in = pltpu.make_async_copy(values.at[me], out_values.at[me], local.at[2])

    def columns(i, width):
        return pl.ds(pl.multiple_of(i * width, width), width)

    def turns(begin, end):
        def body(i, _):
            a = table[:half, columns(i, TILE)]
            table[:half, columns(i, TILE)] = jnp.cos(a)
            table[half:, columns(i, TILE)] = jnp.sin(a)
            return 0

        lax.fori_loop(begin // TILE, end // TILE, body, 0)

    def turn(begin, end):
        def body(i, high):
            block, row = i // (rows // TILE), i % (rows // TILE)
            wide = raw[block, columns(row, TILE), :].astype(jnp.float32).T
            mean = jnp.sum(wide * wide, axis=0, keepdims=True) / size
            wide = wide * lax.rsqrt(mean + 1e-06) * gains[...]
            cosine, sine = table[:half, columns(i, TILE)], table[half:, columns(i, TILE)]
            first, second = wide[:half], wide[half:]
            one = first * cosine - second * sine
            two = second * cosine + first * sine
            table[:half, columns(i, TILE)] = one
            table[half:, columns(i, TILE)] = two
            return jnp.maximum(high, jnp.abs(jnp.concatenate([one, two], axis=0)))

        top[...] = lax.fori_loop(begin // TILE, end // TILE, body, top[...])

    def scale_up():
        high = jnp.broadcast_to(jnp.max(top[...], axis=1, keepdims=True), (size, TILE))
        top[...] = high
        out_scale[...] = high.T[:1]

    def narrow(begin, end):
        def body(i, _):
            out_keys[:, columns(i, TILE)] = (table[:, columns(i, TILE)] / top[...]).astype(jnp.bfloat16)
            return 0

        lax.fori_loop(begin // TILE, end // TILE, body, 0)

    times = hops[-1]["time"] + 1
    at_time = [[i for i, h in enumerate(hops) if h["time"] == t] for t in range(times)]
    third = times // 2
    for t in range(times):
        for i in at_time[t]:
            start(i)
        if t == 0:
            angles_in.start()
            keys_in.start()
            values_in.start()
            gains[...] = jnp.broadcast_to(gain[...], (TILE, size)).T
            top[...] = jnp.zeros_like(top)
            angles_in.wait()
        if t < third:
            turns(t * length // third, (t + 1) * length // third)
        elif t == third + 2:
            keys_in.wait()
            for i, h in enumerate(hops):
                if h["array"] == 0 and h["last"]:
                    arrived(i)
        elif third + 2 < t <= third + 10:
            turn((t - third - 3) * length // 8, (t - third - 2) * length // 8)
        elif t == third + 11:
            scale_up()
        elif third + 11 < t <= third + 19:
            narrow((t - third - 12) * length // 8, (t - third - 11) * length // 8)
    values_in.wait()
    for i in range(len(hops)):
        arrived(i)
    for copy in copies:
        copy.wait_send()


def body(key_rows, value_rows, turn_angle, key_gain):
    blocks, rows, heads, size = key_rows.shape
    length = blocks * rows
    hops, slots = plan()
    strip_rows = rows // len(ORDER)
    vmem, hbm = pl.BlockSpec(memory_space=pltpu.VMEM), pl.BlockSpec(memory_space=pl.ANY)
    stored_keys, stored_values, key_scale = pl.pallas_call(
        functools.partial(kernel, hops),
        name="hand_over",
        out_shape=(
            pltpu.VMEM((size, length), jnp.bfloat16),
            pltpu.VMEM((blocks, rows, size), jnp.bfloat16),
            jax.ShapeDtypeStruct((1, size), jnp.float32),
        ),
        in_specs=[hbm, vmem, hbm, hbm],
        out_specs=(vmem, vmem, vmem),
        scratch_shapes=[
            pltpu.VMEM((blocks, rows, size), jnp.bfloat16),
            pltpu.VMEM((size, length), jnp.float32),
            pltpu.VMEM((slots, strip_rows, size), jnp.bfloat16),
            pltpu.VMEM((size, TILE), jnp.float32),
            pltpu.VMEM((size, TILE), jnp.float32),
            pltpu.SemaphoreType.DMA((len(hops),)),
            pltpu.SemaphoreType.DMA((len(hops),)),
            pltpu.SemaphoreType.DMA((3,)),
        ],
        compiler_params=pltpu.CompilerParams(
            collective_id=0, has_side_effects=True, vmem_limit_bytes=36 << 20
        ),
    )(
        turn_angle.T,
        key_gain.reshape(1, size),
        key_rows.reshape(blocks, rows, size),
        value_rows.reshape(blocks, rows, size),
    )
    return (
        stored_keys.reshape(1, 1, size, length),
        stored_values.reshape(1, length, 1, size),
        key_scale.reshape(1, 1, size),
    )


def solution(mesh):
    return jax.shard_map(
        body,
        mesh=mesh,
        in_specs=(
            P(None, ("block", "span"), "group", None),
            P(None, ("block", "span"), "group", None),
            P(),
            P(),
        ),
        out_specs=(
            P(("block", "span"), "group", None, None),
            P(("block", "span"), None, "group", None),
            P(("block", "span"), "group", None),
        ),
        check_vma=False,
    )
```

time: 212 us -> 153 us (0.72)
  Pallas kernels: 0 us -> 145 us
  waiting for transfers between devices: 118 us -> 0 us
  other arithmetic: 39.3 us -> 0 us
  local copies, waits for them, and re-layouts: 40 us -> 6.57 us
  starting transfers between devices: 12.1 us -> 0 us
    pallas_call x0 -> x1, Pallas kernels: none -> 145 us  [body(): pl.pallas_call(functools.partial(kernel, hops), name='hand_over', out_sha...]
    all_to_all x2 -> x0, waiting for transfers between devices: 118 us -> none  [the longest x1 72.5 us: body(): lax.all_to_all(key_rows, ('block', 'span'), split_axis=0, concat_axis=1,...]
    cos x1 -> x0, local copies, waits for them, and re-layouts: 24.1 us -> none  [apply_rotary(): jnp.cos(angle)[None, :, None, :]]
    all_to_all x2 -> x0, starting transfers between devices: 12.1 us -> none  [the longest x1 7.45 us: body(): lax.all_to_all(key_rows, ('block', 'span'), split_axis=0, concat_axis=1,...]
    sub x1 -> x0, other arithmetic: 11.7 us -> none  [apply_rotary(): first * cosine - second * sine]
    mul x1 -> x0, other arithmetic: 10.5 us -> none  [unit_rows(): vectors * lax.rsqrt(jnp.mean(vectors * vectors, axis=-1, keepdims=True) +...]
    convert_element_type x1 -> x0, local copies, waits for them, and re-layouts: 9.46 us -> none  [ready_to_store(): wide_keys = plain_keys.astype(jnp.float32)]
    transpose x1 -> x0, other arithmetic: 6.93 us -> none  [body(): stored_keys = jnp.transpose(narrow_keys, (0, 2, 3, 1))]
  transfers between devices with their start and end apart: 2 -> 0, of which waited for: 2 -> 0; matrix products, arithmetic and copies ran while one was open for 35% -> 0% of each run, Pallas kernels for 0% -> 0%
where the time goes in v1:
time: 153 us; the launch traced here: 152 us
  Pallas kernels  145 us (95%)
  local copies, waits for them, and re-layouts  6.57 us (4%)
    pallas_call x1, Pallas kernels, body(): pl.pallas_call(functools.partial(kernel, hops), name='hand_over', out_sha...  145 us
    unnamed x5, local copies, waits for them, and re-layouts  6.57 us

profile of v1, /device:TPU:1, one launch (start us, length us, event | category | flops | bytes accessed | tf_op | source)
XLA Modules:
  0.0 151.9 jit_solution(8838929386870381021)
XLA Ops:
  0.6 0.0 copy-start
  0.6 0.6 copy-done
  1.3 144.7 %hand_over.1 = (bf16[128,24576]{1,0:T(8,128)(2,1)S(1)}, bf16[16,1536,128]{2,1,0:T(8,128)(2,1)S(1)}, f32[1,128]{1,0:T(1,128)S(1)}) custom-call(f32[64,24576]{1,0:T(8,128)} %bitcast.11, f32[1,128]{1,0:T(1,128)S(1)} %bitcast.9, bf16[16,1536,128]{2,1,0:T(8,128)(2,1)} %bitcast.12, bf16[16,1536,128]{2,1,0:T(8,128)(2,1)} %bitcast.13), custom_call_target="tpu_custom_call" | custom-call | tf_op jit(solution)/shard_map/hand_over/pallas_call | solution.py:207
  146.0 2.7 %copy.10 = bf16[1,1,128,24576]{3,2,1,0:T(8,128)(2,1)} copy(bf16[1,1,128,24576]{3,2,1,0:T(8,128)(2,1)S(1)} %bitcast.8) | data formatting | bytes 12582912
  148.7 2.7 %copy.11 = bf16[1,24576,1,128]{3,1,2,0:T(8,128)(2,1)} copy(bf16[1,24576,1,128]{3,1,2,0:T(8,128)(2,1)S(1)} %bitcast.7) | data formatting | bytes 12582912
  151.4 0.5 copy.12
Async XLA Ops:
  0.6 0.7 copy-start

commit v2 on v1

v2 whole, which is shorter than its diff:
```python
import functools

import jax
import jax.numpy as jnp
from jax import lax
from jax.experimental import pallas as pl
from jax.experimental.pallas import tpu as pltpu
from jax.sharding import PartitionSpec as P

MESH = pl.DeviceIdType.MESH
STEP = {"x": (1, 0, 0), "z": (0, 0, 1), "p": (0, 1, 0), "m": (0, 3, 0)}
ROUTES = (
    (0, (0, 2, 0), "mm", (2, 8)),
    (0, (1, 1, 0), "px", (2, 8)),
    (0, (0, 1, 0), "p", (9,)),
    (0, (0, 2, 1), "ppz", (0, 4, 9)),
    (0, (1, 0, 1), "zx", (3, 9)),
    (0, (1, 2, 0), "xmm", (0, 4, 9)),
    (0, (0, 3, 1), "zm", (4, 10)),
    (0, (1, 0, 0), "x", (10,)),
    (0, (1, 2, 1), "zxpp", (0, 3, 6, 10)),
    (0, (1, 3, 1), "mxz", (1, 5, 10)),
    (0, (0, 1, 1), "pz", (3, 11)),
    (0, (0, 3, 0), "m", (11,)),
    (0, (1, 1, 1), "zpx", (1, 5, 11)),
    (0, (0, 0, 1), "z", (12,)),
    (0, (1, 3, 0), "mx", (3, 12)),
    (1, (0, 2, 1), "pzp", (1, 7, 11)),
    (1, (0, 1, 0), "p", (12,)),
    (1, (0, 3, 1), "zm", (5, 12)),
    (1, (0, 3, 0), "m", (13,)),
    (1, (1, 0, 1), "xz", (7, 13)),
    (1, (1, 1, 0), "xp", (6, 13)),
    (1, (1, 3, 0), "mx", (7, 13)),
    (1, (0, 1, 1), "pz", (7, 14)),
    (1, (0, 2, 0), "mm", (5, 14)),
    (1, (1, 1, 1), "xzp", (1, 6, 14)),
    (1, (1, 3, 1), "zmx", (2, 6, 14)),
    (1, (0, 0, 1), "z", (15,)),
    (1, (1, 0, 0), "x", (15,)),
    (1, (1, 2, 0), "xpp", (2, 8, 15)),
    (1, (1, 2, 1), "mxzm", (0, 4, 8, 15)),
)
STEPS = 16
AHEAD = 2
TURNS_STEPS = 8
TILE = 128


def plan():
    hops, slots = [], 0
    for array, offset, links, times in ROUTES:
        for at, (link, time) in enumerate(zip(links, times)):
            last = at + 1 == len(links)
            hops.append(
                dict(
                    array=array, offset=offset, at=at, link=link, time=time, done=links[:at],
                    slot=None if last else slots,
                )
            )
            slots += not last
    hops.sort(key=lambda hop: hop["time"])
    where = {(hop["array"], hop["offset"], hop["at"]): i for i, hop in enumerate(hops)}
    for hop in hops:
        hop["after"] = where.get((hop["array"], hop["offset"], hop["at"] - 1))
    return hops, slots


def kernel(
    hops, angle, gain, keys, values, out_keys, out_values, out_scale,
    raw, table, transit, gain_row, gains, top, send, recv, local,
):
    blocks, rows, size = raw.shape
    half = size // 2
    length = blocks * rows
    z = lax.axis_index("block")
    y = lax.axis_index("span") // 2
    x = lax.axis_index("span") % 2

    def device(step):
        return {"block": (z + step[2]) % 2, "span": ((y + step[1]) % 4) * 2 + (x + step[0]) % 2}

    def block_at(dx, dy, dz):
        return ((z + dz) % 2) * 8 + ((y + dy) % 4) * 2 + (x + dx) % 2

    me = block_at(0, 0, 0)
    gain_in = pltpu.make_async_copy(gain, gain_row, local.at[0])
    angles_in = pltpu.make_async_copy(angle, table.at[pl.ds(0, half)], local.at[1])
    keys_in = pltpu.make_async_copy(keys.at[me], raw.at[me], local.at[2])
    values_in = pltpu.make_async_copy(values.at[me], out_values.at[me], local.at[3])

    barrier = pltpu.get_barrier_semaphore()
    for step in STEP.values():
        pl.semaphore_signal(barrier, inc=1, device_id=device(step), device_id_type=MESH)
    pl.semaphore_wait(barrier, len(STEP))

    copies = [None] * len(hops)
    received = set()

    def arrived(i):
        if i not in received:
            copies[i].wait_recv()
            received.add(i)

    def start(i):
        hop = hops[i]
        if hop["after"] is None:
            source = (keys, values)[hop["array"]].at[block_at(*hop["offset"])]
        else:
            arrived(hop["after"])
            source = transit.at[hops[hop["after"]]["slot"]]
        if hop["slot"] is None:
            gone = [sum(STEP[link][axis] for link in hop["done"]) for axis in range(3)]
            target = (raw, out_values)[hop["array"]].at[block_at(gone[0], 8 - gone[1], gone[2])]
        else:
            target = transit.at[hop["slot"]]
        copies[i] = pltpu.make_async_remote_copy(
            src_ref=source,
            dst_ref=target,
            send_sem=send.at[i],
            recv_sem=recv.at[i],
            device_id=device(STEP[hop["link"]]),
            device_id_type=MESH,
        )
        copies[i].start()

    def columns(i):
        return pl.ds(pl.multiple_of(i * TILE, TILE), TILE)

    def turns(begin, end):
        def body(i, _):
            a = table[:half, columns(i)]
            table[:half, columns(i)] = jnp.cos(a)
            table[half:, columns(i)] = jnp.sin(a)
            return 0

        lax.fori_loop(begin, end, body, 0)

    def turn(block):
        def body(i, high):
            at = columns(block * (rows // TILE) + i)
            wide = raw[block, columns(i), :].astype(jnp.float32).T
            mean = jnp.sum(wide * wide, axis=0, keepdims=True) / size
            wide = wide * lax.rsqrt(mean + 1e-06) * gains[...]
            cosine, sine = table[:half, at], table[half:, at]
            first, second = wide[:half], wide[half:]
            one = first * cosine - second * sine
            two = second * cosine + first * sine
            table[:half, at] = one
            table[half:, at] = two
            return jnp.maximum(high, jnp.abs(jnp.concatenate([one, two], axis=0)))

        top[...] = lax.fori_loop(0, rows // TILE, body, top[...])

    def narrow():
        high = jnp.broadcast_to(jnp.max(top[...], axis=1, keepdims=True), (size, TILE))
        top[...] = high
        out_scale[...] = high.T[:1]

        def body(i, _):
            out_keys[:, columns(i)] = (table[:, columns(i)] / top[...]).astype(jnp.bfloat16)
            return 0

        lax.fori_loop(0, length // TILE, body, 0)

    def start_step(time):
        for i, hop in enumerate(hops):
            if hop["time"] == time:
                start(i)

    for time in range(AHEAD):
        start_step(time)
    for copy in (gain_in, angles_in, keys_in, values_in):
        copy.start()
    gain_in.wait()
    gains[...] = jnp.broadcast_to(gain_row[...], (TILE, size)).T
    top[...] = jnp.zeros_like(top)
    angles_in.wait()
    keys_in.wait()
    tiles = length // TILE
    final = [(hop["time"], i) for i, hop in enumerate(hops) if hop["array"] == 0 and hop["slot"] is None]
    for time in range(STEPS):
        start_step(time + AHEAD)
        if time < TURNS_STEPS:
            turns(time * tiles // TURNS_STEPS, (time + 1) * tiles // TURNS_STEPS)
        if time == TURNS_STEPS:
            turn(me)
        for came, i in final:
            if max(came + 1, TURNS_STEPS) == time:
                arrived(i)
                dx, dy, dz = hops[i]["offset"]
                turn(block_at(dx, 4 - dy, dz))
        if time == max(final)[0] + 1:
            narrow()
    values_in.wait()
    for i in range(len(hops)):
        arrived(i)
    for copy in copies:
        copy.wait_send()


def store(keys, values, scale, out_keys, out_values, out_scale, done):
    parts = done.shape[0] // 2
    copies = [pltpu.make_async_copy(scale, out_scale, done.at[2 * parts])]
    for j, (source, target) in enumerate(((keys, out_keys), (values, out_values))):
        step = source.shape[0] // parts
        for i in range(parts):
            part = pl.ds(i * step, step)
            copies.append(
                pltpu.make_async_copy(source.at[part], target.at[part], done.at[j * parts + i])
            )
    for copy in copies:
        copy.start()
    for copy in copies:
        copy.wait()


def body(key_rows, value_rows, turn_angle, key_gain):
    blocks, rows, heads, size = key_rows.shape
    length = blocks * rows
    hops, slots = plan()
    vmem, hbm = pl.BlockSpec(memory_space=pltpu.VMEM), pl.BlockSpec(memory_space=pl.ANY)
    outputs = (
        ((size, length), jnp.bfloat16),
        ((blocks, rows, size), jnp.bfloat16),
        ((1, size), jnp.float32),
    )
    held = pl.pallas_call(
        functools.partial(kernel, hops),
        name="hand_over",
        out_shape=tuple(pltpu.VMEM(*output) for output in outputs),
        in_specs=[hbm, pl.BlockSpec(memory_space=pltpu.HBM), hbm, hbm],
        out_specs=(vmem,) * 3,
        scratch_shapes=[
            pltpu.VMEM((blocks, rows, size), jnp.bfloat16),
            pltpu.VMEM((size, length), jnp.float32),
            pltpu.VMEM((slots, rows, size), jnp.bfloat16),
            pltpu.VMEM((1, size), jnp.float32),
            pltpu.VMEM((size, TILE), jnp.float32),
            pltpu.VMEM((size, TILE), jnp.float32),
            pltpu.SemaphoreType.DMA((len(hops),)),
            pltpu.SemaphoreType.DMA((len(hops),)),
            pltpu.SemaphoreType.DMA((4,)),
        ],
        compiler_params=pltpu.CompilerParams(
            collective_id=0, has_side_effects=True, vmem_limit_bytes=36 << 20
        ),
    )(
        turn_angle.T,
        key_gain.reshape(1, size),
        key_rows.reshape(blocks, rows, size),
        value_rows.reshape(blocks, rows, size),
    )
    stored_keys, stored_values, key_scale = pl.pallas_call(
        store,
        name="store",
        out_shape=tuple(jax.ShapeDtypeStruct(*output) for output in outputs),
        in_specs=[hbm] * 3,
        out_specs=(hbm,) * 3,
        scratch_shapes=[pltpu.SemaphoreType.DMA((9,))],
        compiler_params=pltpu.CompilerParams(vmem_limit_bytes=2 << 20),
    )(*held)
    return (
        stored_keys.reshape(1, 1, size, length),
        stored_values.reshape(1, length, 1, size),
        key_scale.reshape(1, 1, size),
    )


def solution(mesh):
    return jax.shard_map(
        body,
        mesh=mesh,
        in_specs=(
            P(None, ("block", "span"), "group", None),
            P(None, ("block", "span"), "group", None),
            P(),
            P(),
        ),
        out_specs=(
            P(("block", "span"), "group", None, None),
            P(("block", "span"), None, "group", None),
            P(("block", "span"), "group", None),
        ),
        check_vma=False,
    )
```

time: 153 us -> 148 us (0.967)
  local copies, waits for them, and re-layouts: 6.57 us -> 0.65 us
    unnamed x5 -> x2, local copies, waits for them, and re-layouts: 6.57 us -> 0.65 us
    pallas_call x0 -> x1, Pallas kernels: none -> 4.67 us  [body(): pl.pallas_call(store, name='store', out_shape=tuple((jax.ShapeDtypeStruct...]
    pallas_call x1, Pallas kernels: 145 us -> 142 us  [body(): pl.pallas_call(functools.partial(kernel, hops), name='hand_over', out_sha...]
where the time goes in v2:
time: 148 us
  Pallas kernels  146 us (99%)
    pallas_call x1, Pallas kernels, body(): pl.pallas_call(functools.partial(kernel, hops), name='hand_over', out_sha...  142 us
    pallas_call x1, Pallas kernels, body(): pl.pallas_call(store, name='store', out_shape=tuple((jax.ShapeDtypeStruct...  4.67 us

profile of v2, /device:TPU:1, one launch (start us, length us, event | category | flops | bytes accessed | tf_op | source)
XLA Modules:
  0.0 147.6 jit_solution(10985749598634567459)
XLA Ops:
  0.6 0.0 copy-start
  0.6 0.6 copy-done
  1.3 141.6 %hand_over.1 = (bf16[128,24576]{1,0:T(8,128)(2,1)S(1)}, bf16[16,1536,128]{2,1,0:T(8,128)(2,1)S(1)}, f32[1,128]{1,0:T(1,128)S(1)}) custom-call(f32[64,24576]{1,0:T(8,128)} %bitcast.8, f32[1,128]{1,0:T(1,128)S(1)} %bitcast.7, bf16[16,1536,128]{2,1,0:T(8,128)(2,1)} %bitcast.9, bf16[16,1536,128]{2,1,0:T(8,128)(2,1)} %bitcast.10), custom_call_target="tpu_custom_call" | custom-call | tf_op jit(solution)/shard_map/hand_over/pallas_call | solution.py:228
  142.9 4.7 %store.1 = (bf16[128,24576]{1,0:T(8,128)(2,1)}, bf16[16,1536,128]{2,1,0:T(8,128)(2,1)}, f32[1,128]{1,0:T(1,128)}) custom-call(bf16[128,24576]{1,0:T(8,128)(2,1)S(1)} %get-tuple-element.9.keys, bf16[16,1536,128]{2,1,0:T(8,128)(2,1)S(1)} %get-tuple-element.10.values, f32[1,128]{1,0:T(1,128)S(1)} %get-tuple-element.11.scale), custom_call_target="tpu_custom_call" | custom-call | tf_op jit(solution)/shard_map/store/pallas_call | solution.py:254
Async XLA Ops:
  0.6 0.7 copy-start

commit v3 on v2

--- a/solution.py
+++ b/solution.py
@@ -43,8 +43,10 @@
 )
 STEPS = 16
 AHEAD = 2
+SPLIT = 14
 TURNS_STEPS = 8
 TILE = 128
+KEY_PARTS = 4
 
 
 def plan():
@@ -66,22 +68,42 @@
     return hops, slots
 
 
+def late_hops(hops):
+    return [i for i, hop in enumerate(hops) if hop["time"] >= SPLIT]
+
+
+def core():
+    return lax.axis_index("group") % 2
+
+
+def device(step):
+    z, y, x = lax.axis_index("block"), lax.axis_index("span") // 2, lax.axis_index("span") % 2
+    return {"block": (z + step[2]) % 2, "span": ((y + step[1]) % 4) * 2 + (x + step[0]) % 2}
+
+
+def block_at(dx, dy, dz):
+    z, y, x = lax.axis_index("block"), lax.axis_index("span") // 2, lax.axis_index("span") % 2
+    return ((z + dz) % 2) * 8 + ((y + dy) % 4) * 2 + (x + dx) % 2
+
+
+def came_from(offset):
+    return block_at(offset[0], 4 - offset[1], offset[2])
+
+
+def meet():
+    barrier = pltpu.get_barrier_semaphore()
+    for step in STEP.values():
+        pl.semaphore_signal(barrier, inc=1, device_id=device(step), device_id_type=MESH)
+    pl.semaphore_wait(barrier, len(STEP))
+
+
 def kernel(
-    hops, angle, gain, keys, values, out_keys, out_values, out_scale,
-    raw, table, transit, gain_row, gains, top, send, recv, local,
+    hops, angle, gain, keys, values, out_keys, out_values, out_scale, transit,
+    raw, table, gain_row, gains, top, send, recv, local,
 ):
     blocks, rows, size = raw.shape
     half = size // 2
     length = blocks * rows
-    z = lax.axis_index("block")
-    y = lax.axis_index("span") // 2
-    x = lax.axis_index("span") % 2
-
-    def device(step):
-        return {"block": (z + step[2]) % 2, "span": ((y + step[1]) % 4) * 2 + (x + step[0]) % 2}
-
-    def block_at(dx, dy, dz):
-        return ((z + dz) % 2) * 8 + ((y + dy) % 4) * 2 + (x + dx) % 2
 
     me = block_at(0, 0, 0)
     gain_in = pltpu.make_async_copy(gain, gain_row, local.at[0])
@@ -89,11 +111,7 @@
     keys_in = pltpu.make_async_copy(keys.at[me], raw.at[me], local.at[2])
     values_in = pltpu.make_async_copy(values.at[me], out_values.at[me], local.at[3])
 
-    barrier = pltpu.get_barrier_semaphore()
-    for step in STEP.values():
-        pl.semaphore_signal(barrier, inc=1, device_id=device(step), device_id_type=MESH)
-    pl.semaphore_wait(barrier, len(STEP))
-
+    meet()
     copies = [None] * len(hops)
     received = set()
 
@@ -122,7 +140,10 @@
             device_id=device(STEP[hop["link"]]),
             device_id_type=MESH,
         )
-        copies[i].start()
+        if hop["time"] < SPLIT:
+            copies[i].start()
+        else:
+            pl.when(core() == 1)(copies[i].start)
 
     def columns(i):
         return pl.ds(pl.multiple_of(i * TILE, TILE), TILE)
@@ -168,14 +189,15 @@
             if hop["time"] == time:
                 start(i)
 
+    for copy in (gain_in, angles_in, keys_in, values_in):
+        copy.start()
+    pl.when(core() == 1)(angles_in.wait)
     for time in range(AHEAD):
         start_step(time)
-    for copy in (gain_in, angles_in, keys_in, values_in):
-        copy.start()
+    pl.when(core() == 0)(angles_in.wait)
     gain_in.wait()
     gains[...] = jnp.broadcast_to(gain_row[...], (TILE, size)).T
     top[...] = jnp.zeros_like(top)
-    angles_in.wait()
     keys_in.wait()
     tiles = length // TILE
     final = [(hop["time"], i) for i, hop in enumerate(hops) if hop["array"] == 0 and hop["slot"] is None]
@@ -188,53 +210,123 @@
         for came, i in final:
             if max(came + 1, TURNS_STEPS) == time:
                 arrived(i)
-                dx, dy, dz = hops[i]["offset"]
-                turn(block_at(dx, 4 - dy, dz))
+                turn(came_from(hops[i]["offset"]))
         if time == max(final)[0] + 1:
             narrow()
     values_in.wait()
-    for i in range(len(hops)):
-        arrived(i)
-    for copy in copies:
-        copy.wait_send()
-
-
-def store(keys, values, scale, out_keys, out_values, out_scale, done):
-    parts = done.shape[0] // 2
-    copies = [pltpu.make_async_copy(scale, out_scale, done.at[2 * parts])]
-    for j, (source, target) in enumerate(((keys, out_keys), (values, out_values))):
-        step = source.shape[0] // parts
-        for i in range(parts):
-            part = pl.ds(i * step, step)
-            copies.append(
-                pltpu.make_async_copy(source.at[part], target.at[part], done.at[j * parts + i])
+    for i, hop in enumerate(hops):
+        if hop["time"] < SPLIT:
+            arrived(i)
+            copies[i].wait_send()
+
+    @pl.when(core() == 1)
+    def _():
+        for i in late_hops(hops):
+            copies[i].wait()
+
+
+def late(hops, values, transit, _, landed, send, recv):
+    meet()
+
+    @pl.when(core() == 0)
+    def _():
+        copies = []
+        for j, i in enumerate(late_hops(hops)):
+            hop = hops[i]
+            if hop["after"] is None:
+                source = values.at[block_at(*hop["offset"])]
+            else:
+                source = transit.at[hops[hop["after"]]["slot"]]
+            copy = pltpu.make_async_remote_copy(
+                src_ref=source,
+                dst_ref=landed.at[j],
+                send_sem=send.at[j],
+                recv_sem=recv.at[j],
+                device_id=device(STEP[hop["link"]]),
+                device_id_type=MESH,
             )
-    for copy in copies:
+            copy.start()
+            copies.append(copy)
+        for copy in copies:
+            copy.wait()
+
+
+def store(hops, keys, values, scale, out_keys, out_values, out_scale, done):
+    blocks = values.shape[0]
+    part = keys.shape[0] // KEY_PARTS
+    copies = [pltpu.make_async_copy(scale, out_scale, done.at[0])]
+    for i in range(KEY_PARTS):
+        at = pl.ds(i * part, part)
+        copies.append(pltpu.make_async_copy(keys.at[at], out_keys.at[at], done.at[1 + i]))
+    offsets = [hops[i]["offset"] for i in late_hops(hops)]
+    offsets += [(0, 0, 0)] + [
+        hop["offset"] for hop in hops if hop["array"] == 1 and hop["slot"] is None and hop["time"] < SPLIT
+    ]
+    moves = []
+    for i, offset in enumerate(offsets):
+        at = came_from(offset)
+        moves.append(
+            pltpu.make_async_copy(values.at[at], out_values.at[at], done.at[1 + KEY_PARTS + i])
+        )
+    assert len(moves) == blocks
+    later = len(late_hops(hops))
+    for copy in copies + moves[later:]:
         copy.start()
-    for copy in copies:
+
+    @pl.when(core() == 1)
+    def _():
+        for copy in moves[:later]:
+            copy.start()
+        for copy in moves[:later]:
+            copy.wait()
+
+    for copy in copies + moves[later:]:
         copy.wait()
+
+
+def store_late(hops, landed, stored, out_values, done):
+    @pl.when(core() == 0)
+    def _():
+        copies = []
+        for j, i in enumerate(late_hops(hops)):
+            target = out_values.at[came_from(hops[i]["offset"])]
+            copies.append(pltpu.make_async_copy(landed.at[j], target, done.at[j]))
+        for copy in copies:
+            copy.start()
+        for copy in copies:
+            copy.wait()
 
 
 def body(key_rows, value_rows, turn_angle, key_gain):
     blocks, rows, heads, size = key_rows.shape
     length = blocks * rows
     hops, slots = plan()
+    turn_angle, key_gain, key_rows, value_rows = (
+        pltpu.with_memory_space_constraint(array, pltpu.HBM)
+        for array in (
+            turn_angle.T,
+            key_gain.reshape(1, size),
+            key_rows.reshape(blocks, rows, size),
+            value_rows.reshape(blocks, rows, size),
+        )
+    )
     vmem, hbm = pl.BlockSpec(memory_space=pltpu.VMEM), pl.BlockSpec(memory_space=pl.ANY)
     outputs = (
         ((size, length), jnp.bfloat16),
         ((blocks, rows, size), jnp.bfloat16),
         ((1, size), jnp.float32),
     )
-    held = pl.pallas_call(
+    later = len(late_hops(hops))
+    *held, transit = pl.pallas_call(
         functools.partial(kernel, hops),
         name="hand_over",
-        out_shape=tuple(pltpu.VMEM(*output) for output in outputs),
-        in_specs=[hbm, pl.BlockSpec(memory_space=pltpu.HBM), hbm, hbm],
-        out_specs=(vmem,) * 3,
+        out_shape=tuple(pltpu.VMEM(*output) for output in outputs)
+        + (pltpu.VMEM((slots, rows, size), jnp.bfloat16),),
+        in_specs=[hbm] * 4,
+        out_specs=(vmem,) * 4,
         scratch_shapes=[
             pltpu.VMEM((blocks, rows, size), jnp.bfloat16),
             pltpu.VMEM((size, length), jnp.float32),
-            pltpu.VMEM((slots, rows, size), jnp.bfloat16),
             pltpu.VMEM((1, size), jnp.float32),
             pltpu.VMEM((size, TILE), jnp.float32),
             pltpu.VMEM((size, TILE), jnp.float32),
@@ -243,23 +335,39 @@
             pltpu.SemaphoreType.DMA((4,)),
         ],
         compiler_params=pltpu.CompilerParams(
-            collective_id=0, has_side_effects=True, vmem_limit_bytes=36 << 20
+            collective_id=0, has_side_effects=True, vmem_limit_bytes=22 << 20
         ),
-    )(
-        turn_angle.T,
-        key_gain.reshape(1, size),
-        key_rows.reshape(blocks, rows, size),
-        value_rows.reshape(blocks, rows, size),
-    )
+    )(turn_angle, key_gain, key_rows, value_rows)
     stored_keys, stored_values, key_scale = pl.pallas_call(
-        store,
+        functools.partial(store, hops),
         name="store",
         out_shape=tuple(jax.ShapeDtypeStruct(*output) for output in outputs),
         in_specs=[hbm] * 3,
         out_specs=(hbm,) * 3,
-        scratch_shapes=[pltpu.SemaphoreType.DMA((9,))],
-        compiler_params=pltpu.CompilerParams(vmem_limit_bytes=2 << 20),
+        scratch_shapes=[pltpu.SemaphoreType.DMA((1 + KEY_PARTS + blocks,))],
+        compiler_params=pltpu.CompilerParams(vmem_limit_bytes=1 << 20),
     )(*held)
+    landed = pl.pallas_call(
+        functools.partial(late, hops),
+        name="late",
+        out_shape=pltpu.VMEM((later, rows, size), jnp.bfloat16),
+        in_specs=[hbm] * 3,
+        out_specs=vmem,
+        scratch_shapes=[pltpu.SemaphoreType.DMA((later,)), pltpu.SemaphoreType.DMA((later,))],
+        compiler_params=pltpu.CompilerParams(
+            collective_id=1, has_side_effects=True, vmem_limit_bytes=1 << 20
+        ),
+    )(value_rows, transit, pltpu.with_memory_space_constraint(key_scale, pltpu.HBM))
+    stored_values = pl.pallas_call(
+        functools.partial(store_late, hops),
+        name="store_late",
+        out_shape=jax.ShapeDtypeStruct(*outputs[1]),
+        in_specs=[hbm] * 2,
+        out_specs=hbm,
+        scratch_shapes=[pltpu.SemaphoreType.DMA((later,))],
+        input_output_aliases={1: 0},
+        compiler_params=pltpu.CompilerParams(vmem_limit_bytes=1 << 20),
+    )(landed, stored_values)
     return (
         stored_keys.reshape(1, 1, size, length),
         stored_values.reshape(1, length, 1, size),

time: 148 us -> 144 us (0.973)
  Pallas kernels: 146 us -> 142 us
    pallas_call x1, Pallas kernels: 142 us -> 136 us  [body(): pl.pallas_call(functools.partial(kernel, hops), name='hand_over', out_sha...]
    pallas_call x1 -> x3, Pallas kernels: 4.67 us -> 6.31 us  [the longest x1 4.75 us: body(): pl.pallas_call(functools.partial(store, hops), name='store', out_shape=tu...]
where the time goes in v3:
time: 144 us; the launch traced here: 143 us
  Pallas kernels  142 us (99%)
    pallas_call x1, Pallas kernels, body(): pl.pallas_call(functools.partial(kernel, hops), name='hand_over', out_sha...  136 us
    pallas_call x1, Pallas kernels, body(): pl.pallas_call(functools.partial(store, hops), name='store', out_shape=tu...  4.75 us

profile of v3, /device:TPU:1, one launch (start us, length us, event | category | flops | bytes accessed | tf_op | source)
XLA Modules:
  0.0 142.7 jit_solution(4463194045499976986)
XLA Ops:
  0.6 135.7 %hand_over.1 = (bf16[128,24576]{1,0:T(8,128)(2,1)S(1)}, bf16[16,1536,128]{2,1,0:T(8,128)(2,1)S(1)}, f32[1,128]{1,0:T(1,128)S(1)}, bf16[34,1536,128]{2,1,0:T(8,128)(2,1)S(1)}) custom-call(f32[64,24576]{1,0:T(8,128)} %bitcast.9, f32[1,128]{1,0:T(1,128)} %bitcast.13, bf16[16,1536,128]{2,1,0:T(8,128)(2,1)} %bitcast.10, bf16[16,1536,128]{2,1,0:T(8,128)(2,1)} %bitcast.7), custom_call_target="tpu_custom_call" | custom-call | tf_op jit(solution)/shard_map/hand_over/pallas_call | solution.py:320
  136.3 4.8 %store.1 = (bf16[128,24576]{1,0:T(8,128)(2,1)}, bf16[16,1536,128]{2,1,0:T(8,128)(2,1)}, f32[1,128]{1,0:T(1,128)}) custom-call(bf16[128,24576]{1,0:T(8,128)(2,1)S(1)} %get-tuple-element.10.keys, bf16[16,1536,128]{2,1,0:T(8,128)(2,1)S(1)} %get-tuple-element.11.values, f32[1,128]{1,0:T(1,128)S(1)} %get-tuple-element.12.scale), custom_call_target="tpu_custom_call" | custom-call | tf_op jit(solution)/shard_map/store/pallas_call | solution.py:341
  141.1 1.5 %late.1.landed = bf16[8,1536,128]{2,1,0:T(8,128)(2,1)S(1)} custom-call(bf16[16,1536,128]{2,1,0:T(8,128)(2,1)} %bitcast.8, bf16[34,1536,128]{2,1,0:T(8,128)(2,1)S(1)} %get-tuple-element.14.transit, f32[1,128]{1,0:T(1,128)} %get-tuple-element.15._), custom_call_target="tpu_custom_call" | custom-call | tf_op jit(solution)/shard_map/late/pallas_call | solution.py:350
  142.6 0.1 store_late.1

commit v4 on v3

--- a/solution.py
+++ b/solution.py
@@ -43,6 +43,7 @@
 )
 STEPS = 16
 AHEAD = 2
+PAUSES = 1
 SPLIT = 14
 TURNS_STEPS = 8
 TILE = 128
@@ -143,7 +144,7 @@
         if hop["time"] < SPLIT:
             copies[i].start()
         else:
-            pl.when(core() == 1)(copies[i].start)
+            pl.when(core() != PAUSES)(copies[i].start)
 
     def columns(i):
         return pl.ds(pl.multiple_of(i * TILE, TILE), TILE)
@@ -191,10 +192,9 @@
 
     for copy in (gain_in, angles_in, keys_in, values_in):
         copy.start()
-    pl.when(core() == 1)(angles_in.wait)
     for time in range(AHEAD):
         start_step(time)
-    pl.when(core() == 0)(angles_in.wait)
+    angles_in.wait()
     gain_in.wait()
     gains[...] = jnp.broadcast_to(gain_row[...], (TILE, size)).T
     top[...] = jnp.zeros_like(top)
@@ -219,17 +219,16 @@
             arrived(i)
             copies[i].wait_send()
 
-    @pl.when(core() == 1)
+    @pl.when(core() != PAUSES)
     def _():
         for i in late_hops(hops):
             copies[i].wait()
 
 
 def late(hops, values, transit, _, landed, send, recv):
-    meet()
-
-    @pl.when(core() == 0)
+    @pl.when(core() == PAUSES)
     def _():
+        meet()
         copies = []
         for j, i in enumerate(late_hops(hops)):
             hop = hops[i]
@@ -273,7 +272,7 @@
     for copy in copies + moves[later:]:
         copy.start()
 
-    @pl.when(core() == 1)
+    @pl.when(core() != PAUSES)
     def _():
         for copy in moves[:later]:
             copy.start()
@@ -285,7 +284,7 @@
 
 
 def store_late(hops, landed, stored, out_values, done):
-    @pl.when(core() == 0)
+    @pl.when(core() == PAUSES)
     def _():
         copies = []
         for j, i in enumerate(late_hops(hops)):

time: 144 us -> 144 us (level)
    pallas_call x1, Pallas kernels: 1.46 us -> 12.9 us  [body(): pl.pallas_call(functools.partial(late, hops), name='late', out_shape=pltp...]
    pallas_call x1, Pallas kernels: 136 us -> 125 us  [body(): pl.pallas_call(functools.partial(kernel, hops), name='hand_over', out_sha...]
    pallas_call x1, Pallas kernels: 0.09 us -> 1.76 us  [body(): pl.pallas_call(functools.partial(store_late, hops), name='store_late', ou...]
where the time goes in v4:
time: 144 us
  Pallas kernels  143 us (99%)
    pallas_call x1, Pallas kernels, body(): pl.pallas_call(functools.partial(kernel, hops), name='hand_over', out_sha...  125 us
    pallas_call x1, Pallas kernels, body(): pl.pallas_call(functools.partial(late, hops), name='late', out_shape=pltp...  12.9 us
    pallas_call x1, Pallas kernels, body(): pl.pallas_call(functools.partial(store, hops), name='store', out_shape=tu...  3.79 us

profile of v4, /device:TPU:1, one launch (start us, length us, event | category | flops | bytes accessed | tf_op | source)
XLA Modules:
  0.0 143.9 jit_solution(2086638467686265461)
XLA Ops:
  0.6 124.8 %hand_over.1 = (bf16[128,24576]{1,0:T(8,128)(2,1)S(1)}, bf16[16,1536,128]{2,1,0:T(8,128)(2,1)S(1)}, f32[1,128]{1,0:T(1,128)S(1)}, bf16[34,1536,128]{2,1,0:T(8,128)(2,1)S(1)}) custom-call(f32[64,24576]{1,0:T(8,128)} %bitcast.9, f32[1,128]{1,0:T(1,128)} %bitcast.13, bf16[16,1536,128]{2,1,0:T(8,128)(2,1)} %bitcast.10, bf16[16,1536,128]{2,1,0:T(8,128)(2,1)} %bitcast.7), custom_call_target="tpu_custom_call" | custom-call | tf_op jit(solution)/shard_map/hand_over/pallas_call | solution.py:319
  125.4 3.8 %store.1 = (bf16[128,24576]{1,0:T(8,128)(2,1)}, bf16[16,1536,128]{2,1,0:T(8,128)(2,1)}, f32[1,128]{1,0:T(1,128)}) custom-call(bf16[128,24576]{1,0:T(8,128)(2,1)S(1)} %get-tuple-element.10.keys, bf16[16,1536,128]{2,1,0:T(8,128)(2,1)S(1)} %get-tuple-element.11.values, f32[1,128]{1,0:T(1,128)S(1)} %get-tuple-element.12.scale), custom_call_target="tpu_custom_call" | custom-call | tf_op jit(solution)/shard_map/store/pallas_call | solution.py:340
  129.2 12.9 %late.1.landed = bf16[8,1536,128]{2,1,0:T(8,128)(2,1)S(1)} custom-call(bf16[16,1536,128]{2,1,0:T(8,128)(2,1)} %bitcast.8, bf16[34,1536,128]{2,1,0:T(8,128)(2,1)S(1)} %get-tuple-element.14.transit, f32[1,128]{1,0:T(1,128)} %get-tuple-element.15._), custom_call_target="tpu_custom_call" | custom-call | tf_op jit(solution)/shard_map/late/pallas_call | solution.py:349
  142.1 1.8 %store_late.1 = bf16[16,1536,128]{2,1,0:T(8,128)(2,1)} custom-call(bf16[8,1536,128]{2,1,0:T(8,128)(2,1)S(1)} %late.1.landed, bf16[16,1536,128]{2,1,0:T(8,128)(2,1)} %get-tuple-element.16.stored), custom_call_target="tpu_custom_call", output_to_operand_aliasing={{}: (1, {})} | custom-call | tf_op jit(solution)/shard_map/store_late/pallas_call | solution.py:360

commit v5 on v4

--- a/solution.py
+++ b/solution.py
@@ -44,25 +44,28 @@
 STEPS = 16
 AHEAD = 2
 PAUSES = 1
-SPLIT = 14
+SPLIT, EARLY = 14, 768
 TURNS_STEPS = 8
 TILE = 128
 KEY_PARTS = 4
 
 
-def plan():
+def plan(rows):
     hops, slots = [], 0
     for array, offset, links, times in ROUTES:
         for at, (link, time) in enumerate(zip(links, times)):
             last = at + 1 == len(links)
-            hops.append(
-                dict(
-                    array=array, offset=offset, at=at, link=link, time=time, done=links[:at],
-                    slot=None if last else slots,
+            parts = [(0, EARLY), (EARLY, rows - EARLY)] if time == SPLIT else [(0, rows)]
+            for begin, count in parts:
+                hops.append(
+                    dict(
+                        array=array, offset=offset, at=at, link=link, time=time, done=links[:at],
+                        slot=None if last else slots, begin=begin, count=count,
+                        late=time > SPLIT or (time == SPLIT and begin > 0),
+                    )
                 )
-            )
             slots += not last
-    hops.sort(key=lambda hop: hop["time"])
+    hops.sort(key=lambda hop: (hop["time"], hop["begin"]))
     where = {(hop["array"], hop["offset"], hop["at"]): i for i, hop in enumerate(hops)}
     for hop in hops:
         hop["after"] = where.get((hop["array"], hop["offset"], hop["at"] - 1))
@@ -70,7 +73,11 @@
 
 
 def late_hops(hops):
-    return [i for i, hop in enumerate(hops) if hop["time"] >= SPLIT]
+    return [i for i, hop in enumerate(hops) if hop["late"]]
+
+
+def part(hop):
+    return pl.ds(hop["begin"], hop["count"])
 
 
 def core():
@@ -124,15 +131,17 @@
     def start(i):
         hop = hops[i]
         if hop["after"] is None:
-            source = (keys, values)[hop["array"]].at[block_at(*hop["offset"])]
+            source = (keys, values)[hop["array"]].at[block_at(*hop["offset"]), part(hop)]
         else:
             arrived(hop["after"])
-            source = transit.at[hops[hop["after"]]["slot"]]
+            source = transit.at[hops[hop["after"]]["slot"], part(hop)]
         if hop["slot"] is None:
             gone = [sum(STEP[link][axis] for link in hop["done"]) for axis in range(3)]
-            target = (raw, out_values)[hop["array"]].at[block_at(gone[0], 8 - gone[1], gone[2])]
+            target = (raw, out_values)[hop["array"]].at[
+                block_at(gone[0], 8 - gone[1], gone[2]), part(hop)
+            ]
         else:
-            target = transit.at[hop["slot"]]
+            target = transit.at[hop["slot"], part(hop)]
         copies[i] = pltpu.make_async_remote_copy(
             src_ref=source,
             dst_ref=target,
@@ -141,10 +150,10 @@
             device_id=device(STEP[hop["link"]]),
             device_id_type=MESH,
         )
-        if hop["time"] < SPLIT:
+        if hop["late"]:
+            pl.when(core() != PAUSES)(copies[i].start)
+        else:
             copies[i].start()
-        else:
-            pl.when(core() != PAUSES)(copies[i].start)
 
     def columns(i):
         return pl.ds(pl.multiple_of(i * TILE, TILE), TILE)
@@ -192,9 +201,10 @@
 
     for copy in (gain_in, angles_in, keys_in, values_in):
         copy.start()
+    pl.when(core() != PAUSES)(angles_in.wait)
     for time in range(AHEAD):
         start_step(time)
-    angles_in.wait()
+    pl.when(core() == PAUSES)(angles_in.wait)
     gain_in.wait()
     gains[...] = jnp.broadcast_to(gain_row[...], (TILE, size)).T
     top[...] = jnp.zeros_like(top)
@@ -215,7 +225,7 @@
             narrow()
     values_in.wait()
     for i, hop in enumerate(hops):
-        if hop["time"] < SPLIT:
+        if not hop["late"]:
             arrived(i)
             copies[i].wait_send()
 
@@ -233,12 +243,12 @@
         for j, i in enumerate(late_hops(hops)):
             hop = hops[i]
             if hop["after"] is None:
-                source = values.at[block_at(*hop["offset"])]
+                source = values.at[block_at(*hop["offset"]), part(hop)]
             else:
-                source = transit.at[hops[hop["after"]]["slot"]]
+                source = transit.at[hops[hop["after"]]["slot"], part(hop)]
             copy = pltpu.make_async_remote_copy(
                 src_ref=source,
-                dst_ref=landed.at[j],
+                dst_ref=landed.at[j, part(hop)],
                 send_sem=send.at[j],
                 recv_sem=recv.at[j],
                 device_id=device(STEP[hop["link"]]),
@@ -251,23 +261,21 @@
 
 
 def store(hops, keys, values, scale, out_keys, out_values, out_scale, done):
-    blocks = values.shape[0]
-    part = keys.shape[0] // KEY_PARTS
+    size = keys.shape[0] // KEY_PARTS
     copies = [pltpu.make_async_copy(scale, out_scale, done.at[0])]
     for i in range(KEY_PARTS):
-        at = pl.ds(i * part, part)
+        at = pl.ds(i * size, size)
         copies.append(pltpu.make_async_copy(keys.at[at], out_keys.at[at], done.at[1 + i]))
-    offsets = [hops[i]["offset"] for i in late_hops(hops)]
-    offsets += [(0, 0, 0)] + [
-        hop["offset"] for hop in hops if hop["array"] == 1 and hop["slot"] is None and hop["time"] < SPLIT
-    ]
+    own = dict(offset=(0, 0, 0), begin=0, count=values.shape[1])
+    final = [hop for hop in hops if hop["array"] == 1 and hop["slot"] is None and not hop["late"]]
     moves = []
-    for i, offset in enumerate(offsets):
-        at = came_from(offset)
+    for i, hop in enumerate([hops[i] for i in late_hops(hops)] + [own] + final):
+        at = came_from(hop["offset"])
         moves.append(
-            pltpu.make_async_copy(values.at[at], out_values.at[at], done.at[1 + KEY_PARTS + i])
+            pltpu.make_async_copy(
+                values.at[at, part(hop)], out_values.at[at, part(hop)], done.at[1 + KEY_PARTS + i]
+            )
         )
-    assert len(moves) == blocks
     later = len(late_hops(hops))
     for copy in copies + moves[later:]:
         copy.start()
@@ -288,8 +296,9 @@
     def _():
         copies = []
         for j, i in enumerate(late_hops(hops)):
-            target = out_values.at[came_from(hops[i]["offset"])]
-            copies.append(pltpu.make_async_copy(landed.at[j], target, done.at[j]))
+            rows = part(hops[i])
+            target = out_values.at[came_from(hops[i]["offset"]), rows]
+            copies.append(pltpu.make_async_copy(landed.at[j, rows], target, done.at[j]))
         for copy in copies:
             copy.start()
         for copy in copies:
@@ -299,7 +308,7 @@
 def body(key_rows, value_rows, turn_angle, key_gain):
     blocks, rows, heads, size = key_rows.shape
     length = blocks * rows
-    hops, slots = plan()
+    hops, slots = plan(rows)
     turn_angle, key_gain, key_rows, value_rows = (
         pltpu.with_memory_space_constraint(array, pltpu.HBM)
         for array in (
@@ -343,7 +352,7 @@
         out_shape=tuple(jax.ShapeDtypeStruct(*output) for output in outputs),
         in_specs=[hbm] * 3,
         out_specs=(hbm,) * 3,
-        scratch_shapes=[pltpu.SemaphoreType.DMA((1 + KEY_PARTS + blocks,))],
+        scratch_shapes=[pltpu.SemaphoreType.DMA((1 + KEY_PARTS + blocks + len(hops),))],
         compiler_params=pltpu.CompilerParams(vmem_limit_bytes=1 << 20),
     )(*held)
     landed = pl.pallas_call(

time: 144 us -> 144 us (level)
    pallas_call x1, Pallas kernels: 12.9 us -> 10.5 us  [body(): pl.pallas_call(functools.partial(late, hops), name='late', out_shape=pltp...]
    pallas_call x1, Pallas kernels: 125 us -> 126 us  [body(): pl.pallas_call(functools.partial(kernel, hops), name='hand_over', out_sha...]
where the time goes in v5:
time: 144 us
  Pallas kernels  143 us (99%)
    pallas_call x1, Pallas kernels, body(): pl.pallas_call(functools.partial(kernel, hops), name='hand_over', out_sha...  126 us
    pallas_call x1, Pallas kernels, body(): pl.pallas_call(functools.partial(late, hops), name='late', out_shape=pltp...  10.5 us
    pallas_call x1, Pallas kernels, body(): pl.pallas_call(functools.partial(store, hops), name='store', out_shape=tu...  4.62 us

profile of v5, /device:TPU:1, one launch (start us, length us, event | category | flops | bytes accessed | tf_op | source)
XLA Modules:
  0.0 143.6 jit_solution(13132345538247249244)
XLA Ops:
  0.6 126.3 %hand_over.1 = (bf16[128,24576]{1,0:T(8,128)(2,1)S(1)}, bf16[16,1536,128]{2,1,0:T(8,128)(2,1)S(1)}, f32[1,128]{1,0:T(1,128)S(1)}, bf16[34,1536,128]{2,1,0:T(8,128)(2,1)S(1)}) custom-call(f32[64,24576]{1,0:T(8,128)} %bitcast.9, f32[1,128]{1,0:T(1,128)} %bitcast.13, bf16[16,1536,128]{2,1,0:T(8,128)(2,1)} %bitcast.10, bf16[16,1536,128]{2,1,0:T(8,128)(2,1)} %bitcast.7), custom_call_target="tpu_custom_call" | custom-call | tf_op jit(solution)/shard_map/hand_over/pallas_call | solution.py:328
  126.9 4.6 %store.1 = (bf16[128,24576]{1,0:T(8,128)(2,1)}, bf16[16,1536,128]{2,1,0:T(8,128)(2,1)}, f32[1,128]{1,0:T(1,128)}) custom-call(bf16[128,24576]{1,0:T(8,128)(2,1)S(1)} %get-tuple-element.10.keys, bf16[16,1536,128]{2,1,0:T(8,128)(2,1)S(1)} %get-tuple-element.11.values, f32[1,128]{1,0:T(1,128)S(1)} %get-tuple-element.12.scale), custom_call_target="tpu_custom_call" | custom-call | tf_op jit(solution)/shard_map/store/pallas_call | solution.py:349
  131.6 10.5 %late.1.landed = bf16[8,1536,128]{2,1,0:T(8,128)(2,1)S(1)} custom-call(bf16[16,1536,128]{2,1,0:T(8,128)(2,1)} %bitcast.8, bf16[34,1536,128]{2,1,0:T(8,128)(2,1)S(1)} %get-tuple-element.14.transit, f32[1,128]{1,0:T(1,128)} %get-tuple-element.15._), custom_call_target="tpu_custom_call" | custom-call | tf_op jit(solution)/shard_map/late/pallas_call | solution.py:358
  142.1 1.5 %store_late.1 = bf16[16,1536,128]{2,1,0:T(8,128)(2,1)} custom-call(bf16[8,1536,128]{2,1,0:T(8,128)(2,1)S(1)} %late.1.landed, bf16[16,1536,128]{2,1,0:T(8,128)(2,1)} %get-tuple-element.16.stored), custom_call_target="tpu_custom_call", output_to_operand_aliasing={{}: (1, {})} | custom-call | tf_op jit(solution)/shard_map/store_late/pallas_call | solution.py:369

commit v6 on v5

--- a/solution.py
+++ b/solution.py
@@ -76,6 +76,10 @@
     return [i for i, hop in enumerate(hops) if hop["late"]]
 
 
+def early_values(hops):
+    return [hop for hop in hops if hop["array"] == 1 and hop["slot"] is None and not hop["late"]]
+
+
 def part(hop):
     return pl.ds(hop["begin"], hop["count"])
 
@@ -267,27 +271,33 @@
         at = pl.ds(i * size, size)
         copies.append(pltpu.make_async_copy(keys.at[at], out_keys.at[at], done.at[1 + i]))
     own = dict(offset=(0, 0, 0), begin=0, count=values.shape[1])
-    final = [hop for hop in hops if hop["array"] == 1 and hop["slot"] is None and not hop["late"]]
     moves = []
-    for i, hop in enumerate([hops[i] for i in late_hops(hops)] + [own] + final):
+    for i, hop in enumerate([own] + early_values(hops)):
         at = came_from(hop["offset"])
         moves.append(
             pltpu.make_async_copy(
                 values.at[at, part(hop)], out_values.at[at, part(hop)], done.at[1 + KEY_PARTS + i]
             )
         )
-    later = len(late_hops(hops))
-    for copy in copies + moves[later:]:
+    step = values.shape[0] // KEY_PARTS
+    whole = []
+    for i in range(KEY_PARTS):
+        at = pl.ds(i * step, step)
+        whole.append(
+            pltpu.make_async_copy(values.at[at], out_values.at[at], done.at[1 + KEY_PARTS + i])
+        )
+    for copy in copies:
         copy.start()
-
-    @pl.when(core() != PAUSES)
-    def _():
-        for copy in moves[:later]:
-            copy.start()
-        for copy in moves[:later]:
-            copy.wait()
-
-    for copy in copies + moves[later:]:
+    for mine, group in ((core() == PAUSES, moves), (core() != PAUSES, whole)):
+
+        @pl.when(mine)
+        def _(group=group):
+            for copy in group:
+                copy.start()
+            for copy in group:
+                copy.wait()
+
+    for copy in copies:
         copy.wait()
 
 
@@ -352,7 +362,7 @@
         out_shape=tuple(jax.ShapeDtypeStruct(*output) for output in outputs),
         in_specs=[hbm] * 3,
         out_specs=(hbm,) * 3,
-        scratch_shapes=[pltpu.SemaphoreType.DMA((1 + KEY_PARTS + blocks + len(hops),))],
+        scratch_shapes=[pltpu.SemaphoreType.DMA((2 + KEY_PARTS + len(early_values(hops)),))],
         compiler_params=pltpu.CompilerParams(vmem_limit_bytes=1 << 20),
     )(*held)
     landed = pl.pallas_call(

time: 144 us -> 144 us (level)
  no operation moved by 1% of the time
where the time goes in v6:
time: 144 us
  Pallas kernels  143 us (99%)
    pallas_call x1, Pallas kernels, body(): pl.pallas_call(functools.partial(kernel, hops), name='hand_over', out_sha...  126 us
    pallas_call x1, Pallas kernels, body(): pl.pallas_call(functools.partial(late, hops), name='late', out_shape=pltp...  11.2 us
    pallas_call x1, Pallas kernels, body(): pl.pallas_call(functools.partial(store, hops), name='store', out_shape=tu...  3.99 us

profile of v6, /device:TPU:1, one launch (start us, length us, event | category | flops | bytes accessed | tf_op | source)
XLA Modules:
  0.0 143.6 jit_solution(10789682210830274465)
XLA Ops:
  0.6 126.3 %hand_over.1 = (bf16[128,24576]{1,0:T(8,128)(2,1)S(1)}, bf16[16,1536,128]{2,1,0:T(8,128)(2,1)S(1)}, f32[1,128]{1,0:T(1,128)S(1)}, bf16[34,1536,128]{2,1,0:T(8,128)(2,1)S(1)}) custom-call(f32[64,24576]{1,0:T(8,128)} %bitcast.9, f32[1,128]{1,0:T(1,128)} %bitcast.13, bf16[16,1536,128]{2,1,0:T(8,128)(2,1)} %bitcast.10, bf16[16,1536,128]{2,1,0:T(8,128)(2,1)} %bitcast.7), custom_call_target="tpu_custom_call" | custom-call | tf_op jit(solution)/shard_map/hand_over/pallas_call | solution.py:338
  126.9 4.0 %store.1 = (bf16[128,24576]{1,0:T(8,128)(2,1)}, bf16[16,1536,128]{2,1,0:T(8,128)(2,1)}, f32[1,128]{1,0:T(1,128)}) custom-call(bf16[128,24576]{1,0:T(8,128)(2,1)S(1)} %get-tuple-element.10.keys, bf16[16,1536,128]{2,1,0:T(8,128)(2,1)S(1)} %get-tuple-element.11.values, f32[1,128]{1,0:T(1,128)S(1)} %get-tuple-element.12.scale), custom_call_target="tpu_custom_call" | custom-call | tf_op jit(solution)/shard_map/store/pallas_call | solution.py:359
  130.9 11.2 %late.1.landed = bf16[8,1536,128]{2,1,0:T(8,128)(2,1)S(1)} custom-call(bf16[16,1536,128]{2,1,0:T(8,128)(2,1)} %bitcast.8, bf16[34,1536,128]{2,1,0:T(8,128)(2,1)S(1)} %get-tuple-element.14.transit, f32[1,128]{1,0:T(1,128)} %get-tuple-element.15._), custom_call_target="tpu_custom_call" | custom-call | tf_op jit(solution)/shard_map/late/pallas_call | solution.py:368
  142.1 1.5 %store_late.1 = bf16[16,1536,128]{2,1,0:T(8,128)(2,1)} custom-call(bf16[8,1536,128]{2,1,0:T(8,128)(2,1)S(1)} %late.1.landed, bf16[16,1536,128]{2,1,0:T(8,128)(2,1)} %get-tuple-element.16.stored), custom_call_target="tpu_custom_call", output_to_operand_aliasing={{}: (1, {})} | custom-call | tf_op jit(solution)/shard_map/store_late/pallas_call | solution.py:379
